TPU v7x, 32 devices: a whole 2x2x4 slice. The times are simulated.
32 devices in a mesh: blk: 8 (over y, x, core), lvl: 4 (over z).
Axes of the slice: x: 2, y: 2, z: 4, core: 2. Of those that a mesh axis runs over, the one named last changes fastest.
Arguments:
- vorticity: bfloat16 [4, 3, 64, 32768], P('lvl', None, 'blk'), may hold values from -6 to 6
- shift_field: bfloat16 [4, 64, 32768], P('lvl', 'blk'), may hold values from -0.8984375 to 0.8984375
- new_index: int32 [4, 64], P('lvl', 'blk'), may hold values from 0 to 63, as said below
- parent_slot: int32 [4, 64], P('lvl', 'blk'), may hold values from 0 to 511, as said below
- flags: int32 [4, 64], P('lvl', 'blk'), may hold values 0 or 1
Outputs:
- field: bfloat16 [4, 3, 64, 32768], P('lvl', None, 'blk')
Inputs may be any that keep to these rules, and one draw needn't show every extreme that they name: `new_index`: in each level a permutation of the block positions; position b lies on device b // 8 of blk. No device sends more than 2 of its blocks to one device, and that number is reached. `parent_slot`: in each level all values differ; value // 8 is a block of the next coarser level and lies on device value // 64. No device has more than 2 blocks whose parents lie on one device, counting the blocks it holds before migration or those it holds after, and that number is reached in both. The values of level 0 are not used.
All inputs are finite; a program needn't handle non-finite values. No bound on the sum of `flags` on one device may be relied on, other than what follows from the above.
Results may differ from a plain program's by a relative error of at most 0.001.
Values may be sent and summed in bfloat16 or wider, within the bound.
A program may use at most 128 MiB of HBM per device.

v0:
```python
import functools

import jax
import jax.numpy as jnp
import numpy as np
from jax import lax
from jax.experimental import pallas as pl
from jax.experimental.pallas import tpu as pltpu
from jax.sharding import PartitionSpec as P

MESH = pl.DeviceIdType.MESH
EDGE = 32
PLANE = EDGE * EDGE
HALO = 2 * PLANE
CAP = 2
VMEM_LIMIT = 60 * 1024 * 1024


def device(blk, lvl):
    return {"blk": blk, "lvl": lvl}


def enter(n, levels, me, lvl):
    barrier = pltpu.get_barrier_semaphore()

    def greet(blk, level):
        pl.semaphore_signal(barrier, inc=1, device_id=device(blk, level), device_id_type=MESH)

    for k in range(1, n):
        greet(lax.rem(me + k, n), lvl)

    @pl.when(lvl > 0)
    def _():
        for k in range(n):
            greet(lax.rem(me + k, n), lvl - 1)

    @pl.when(lvl < levels - 1)
    def _():
        for k in range(n):
            greet(lax.rem(me + k, n), lvl + 1)

    pl.semaphore_wait(
        barrier, n - 1 + n * ((lvl > 0).astype(jnp.int32) + (lvl < levels - 1).astype(jnp.int32))
    )


def remote(src, dst, send, recv, target):
    return pltpu.make_async_remote_copy(
        src_ref=src, dst_ref=dst, send_sem=send, recv_sem=recv, device_id=target, device_id_type=MESH
    )


def share_kernel(n, levels, tab, vort, shift, below_v, below_s, above_v, above_s, tables,
                 near_s, near_r, coarse_s, coarse_r, halo_s, halo_r):
    me = lax.axis_index("blk")
    lvl = lax.axis_index("lvl")
    cells = vort.shape[2]
    enter(n, levels, me, lvl)

    def high(target):
        part = pl.ds(cells - HALO, HALO)
        return (
            remote(vort.at[:, :, part], below_v, halo_s.at[0], halo_r.at[0], target),
            remote(shift.at[:, part], below_s, halo_s.at[1], halo_r.at[1], target),
        )

    def low(target):
        part = pl.ds(0, HALO)
        return (
            remote(vort.at[:, :, part], above_v, halo_s.at[2], halo_r.at[2], target),
            remote(shift.at[:, part], above_s, halo_s.at[3], halo_r.at[3], target),
        )

    after = device(lax.rem(me + 1, n), lvl)
    before = device(lax.rem(me + n - 1, n), lvl)

    @pl.when(me < n - 1)
    def _():
        for copy in high(after):
            copy.start()

    @pl.when(me > 0)
    def _():
        for copy in low(before):
            copy.start()

    near = [
        remote(tab, tables.at[0, me], near_s.at[k], near_r.at[k], device(lax.rem(me + k, n), lvl))
        for k in range(1, n)
    ]
    for copy in near:
        copy.start()
    coarse_level = jnp.maximum(lvl - 1, 0)

    @pl.when(lvl > 0)
    def _():
        for k in range(n):
            remote(tab, tables.at[1, me], coarse_s.at[k], coarse_r.at[k],
                   device(lax.rem(me + k, n), coarse_level)).start()

    tables[0, me] = tab[...]
    for k in range(1, n):
        source = lax.rem(me + n - k, n)
        remote(tab, tables.at[0, source], near_s.at[k], near_r.at[k], before).wait_recv()
        near[k - 1].wait_send()

    @pl.when(lvl > 0)
    def _():
        for k in range(n):
            remote(tab, tables.at[1, me], coarse_s.at[k], coarse_r.at[k],
                   device(lax.rem(me + k, n), coarse_level)).wait_send()

    @pl.when(lvl < levels - 1)
    def _():
        for k in range(n):
            source = lax.rem(me + n - k, n)
            remote(tab, tables.at[1, source], coarse_s.at[k], coarse_r.at[k], before).wait_recv()

    @pl.when(me < n - 1)
    def _():
        for copy in high(after):
            copy.wait_send()
        for copy in low(after):
            copy.wait_recv()

    @pl.when(me > 0)
    def _():
        for copy in low(before):
            copy.wait_send()
        for copy in high(before):
            copy.wait_recv()


def tap_weights(shifts):
    size = jnp.abs(shifts)
    rest = 1.0 - size
    size2 = size * size
    rest2 = rest * rest
    middle = 1.0 + size2 * (1.5 * size - 2.5)
    ahead = 1.0 + rest2 * (1.5 * rest - 2.5)
    behind = -0.5 * rest2 * size
    far = -0.5 * size2 * rest
    up = shifts >= 0.0
    return {
        -2: jnp.where(up, 0.0, far),
        -1: jnp.where(up, behind, ahead),
        0: middle,
        1: jnp.where(up, ahead, behind),
        2: jnp.where(up, far, 0.0),
    }


def remesh_kernel(n, tables, vort, shift, below_v, below_s, above_v, above_s, shrink, send, ghost, rows):
    me = lax.axis_index("blk")
    blocks = vort.shape[1]
    lane_tiles = PLANE // 128
    sublane = lax.broadcasted_iota(jnp.int32, (blocks, 128), 0)

    def tile(ref, c, at):
        part = ref[c, :, pl.ds(at, 128)] if c is not None else ref[:, pl.ds(at, 128)]
        return part.astype(jnp.float32)

    def source_tile(own, low, high, c, x, j):
        if 0 <= x < EDGE:
            return tile(own, c, pl.multiple_of(x * PLANE + j * 128, 128))
        if x < 0:
            inner = pltpu.roll(tile(own, c, pl.multiple_of((EDGE + x) * PLANE + j * 128, 128)), 1, 0)
            outer = pltpu.roll(tile(low, c, pl.multiple_of((2 + x) * PLANE + j * 128, 128)), 1, 0)
            outer = jnp.where(me == 0, 0.0, outer)
            return jnp.where(sublane == 0, outer, inner)
        inner = pltpu.roll(tile(own, c, pl.multiple_of((x - EDGE) * PLANE + j * 128, 128)), blocks - 1, 0)
        outer = pltpu.roll(tile(high, c, pl.multiple_of((x - EDGE) * PLANE + j * 128, 128)), blocks - 1, 0)
        outer = jnp.where(me == n - 1, 0.0, outer)
        return jnp.where(sublane == blocks - 1, outer, inner)

    def chunk(j, carry):
        sums = {}
        for x in range(-2, EDGE + 2):
            weights = tap_weights(source_tile(shift, below_s, above_s, None, x, j))
            for c in range(3):
                value = source_tile(vort, below_v, above_v, c, x, j)
                for offset in range(-2, 3):
                    to = x + offset
                    if 0 <= to < EDGE:
                        term = value * weights[offset]
                        sums[to, c] = sums[to, c] + term if (to, c) in sums else term
            done = x - 2
            if 0 <= done < EDGE:
                for c in range(3):
                    at = pl.multiple_of((done * lane_tiles + j) * blocks, blocks)
                    rows[c, pl.ds(at, blocks), :] = sums.pop((done, c))
        return carry

    lax.fori_loop(0, lane_tiles, chunk, 0)

    height = rows.shape[1] // blocks
    quarter = height // 4
    owners, parents = [], []
    for b in range(blocks):
        position = tables[0, me, 0, b]
        home = lax.div(position, blocks)
        parent = tables[0, home, 0, blocks + lax.rem(position, blocks)]
        parent_owner = lax.div(parent, 8 * blocks)
        rank = sum([(home == other).astype(jnp.int32) for other in owners], jnp.int32(0))
        parent_rank = sum([(parent_owner == other).astype(jnp.int32) for other in parents], jnp.int32(0))
        owners.append(home)
        parents.append(parent_owner)
        for c in range(3):
            block = rows[c, pl.ds(b, height, stride=blocks), :].astype(jnp.bfloat16)
            send[home, rank, c] = block
            wide = jnp.concatenate([block[q * quarter:(q + 1) * quarter] for q in range(4)], axis=1)
            pairs = jnp.dot(wide, shrink[...], preferred_element_type=jnp.float32)
            pairs = pairs.reshape(4, 2, 8, 128)
            ghost[parent_owner, parent_rank, c] = (
                (pairs[:, 0] + pairs[:, 1]).reshape(32, 128).astype(jnp.bfloat16)
            )


def exchange_kernel(n, levels, send, ghost, got, got_ghost, near_s, near_r, coarse_s, coarse_r):
    me = lax.axis_index("blk")
    lvl = lax.axis_index("lvl")
    coarse_level = jnp.maximum(lvl - 1, 0)
    enter(n, levels, me, lvl)

    def near(k):
        to = lax.rem(me + k, n)
        return remote(send.at[to], got.at[me], near_s.at[k], near_r.at[k], device(to, lvl))

    def coarse(k):
        to = lax.rem(me + k, n)
        return remote(ghost.at[to], got_ghost.at[me], coarse_s.at[k], coarse_r.at[k],
                      device(to, coarse_level))

    for k in range(1, n):
        near(k).start()

    @pl.when(lvl > 0)
    def _():
        for k in range(n):
            coarse(k).start()

    before = device(lax.rem(me + n - 1, n), lvl)
    for k in range(1, n):
        source = lax.rem(me + n - k, n)
        remote(send.at[me], got.at[source], near_s.at[k], near_r.at[k], before).wait_recv()

    @pl.when(lvl < levels - 1)
    def _():
        for k in range(n):
            source = lax.rem(me + n - k, n)
            remote(ghost.at[me], got_ghost.at[source], coarse_s.at[k], coarse_r.at[k], before).wait_recv()

    for k in range(1, n):
        near(k).wait_send()

    @pl.when(lvl > 0)
    def _():
        for k in range(n):
            coarse(k).wait_send()


def settle_kernel(n, levels, tables, send, got, got_ghost, grow, out, rows):
    me = lax.axis_index("blk")
    lvl = lax.axis_index("lvl")
    blocks = out.shape[1]
    height = rows.shape[1] // blocks

    def place(e, count):
        source = lax.div(e, blocks)
        b = lax.rem(e, blocks)
        count = jnp.where(b == 0, 0, count)
        position = tables[0, source, 0, b]
        mine = lax.div(position, blocks) == me
        spot = lax.rem(position, blocks)

        def put(ref):
            for c in range(3):
                rows[c, pl.ds(spot, height, stride=blocks), :] = ref[source, count, c].astype(jnp.float32)

        @pl.when(jnp.logical_and(mine, source == me))
        def _():
            put(send)

        @pl.when(jnp.logical_and(mine, source != me))
        def _():
            put(got)

        return count + mine.astype(jnp.int32)

    lax.fori_loop(0, n * blocks, place, jnp.int32(0))

    row = lax.broadcasted_iota(jnp.int32, (32, 32), 0)
    column = lax.broadcasted_iota(jnp.int32, (32, 32), 1)
    mask_row = lax.broadcasted_iota(jnp.int32, (32, 128), 0)
    mask_lane = lax.broadcasted_iota(jnp.int32, (32, 128), 1)

    def refine(e, count):
        source = lax.div(e, blocks)
        b = lax.rem(e, blocks)
        count = jnp.where(b == 0, 0, count)
        position = tables[1, source, 0, b]
        home = lax.div(position, blocks)
        local = lax.rem(position, blocks)
        parent = tables[1, home, 0, blocks + local]
        flag = tables[1, home, 0, 2 * blocks + local]
        mine = lax.div(parent, 8 * blocks) == me

        @pl.when(jnp.logical_and(mine, flag == 1))
        def _():
            code = lax.rem(parent, 8 * blocks)
            spot = lax.div(code, 8)
            ox = lax.rem(lax.div(code, 4), 2)
            oy = lax.rem(lax.div(code, 2), 2)
            oz = lax.rem(code, 2)
            spread = []
            for half in range(2):
                hot = jnp.logical_and(row // 8 == column // 8,
                                      column % 8 == 2 * (row % 8 - 4 * oy) + half)
                spread.append(hot.astype(jnp.float32).astype(jnp.bfloat16))
            mask = jnp.logical_and(mask_row % 8 // 4 == oy, mask_lane % 32 // 16 == oz)
            for c in range(3):
                block = got_ghost[source, count, c]
                wide = jnp.concatenate(
                    [jnp.dot(part, block, preferred_element_type=jnp.float32) for part in spread], axis=1
                ).astype(jnp.bfloat16)
                full = jnp.dot(wide, grow[oz], preferred_element_type=jnp.float32)
                for q in range(4):
                    where = pl.ds((ox * 128 + q * 32) * blocks + spot, 32, stride=blocks)
                    rows[c, where, :] = jnp.where(
                        mask, full[:, q * 128:(q + 1) * 128], rows[c, where, :]
                    )

        return count + mine.astype(jnp.int32)

    lax.fori_loop(0, jnp.where(lvl < levels - 1, n * blocks, 0), refine, jnp.int32(0))

    def finish(r, carry):
        for c in range(3):
            for step in range(8):
                at = r * 8 + step
                out[c, :, pl.ds(pl.multiple_of(at * 128, 128), 128)] = rows[
                    c, pl.ds(pl.multiple_of(at * blocks, blocks), blocks), :
                ].astype(jnp.bfloat16)
        return carry

    lax.fori_loop(0, height // 8, finish, 0)


def selection_tables():
    src = np.arange(512)
    to = np.arange(128)
    q, y, z = src // 128, src % 128 // 32, src % 32
    target = q * 32 + (y // 2) * 16 + z // 2
    shrink = np.where(target[:, None] == to[None, :], 0.125, 0.0)
    part = np.arange(256)
    half, pq, py, pz = part // 128, part % 128 // 32, part % 32 // 16, part % 16
    grow = np.zeros((2, 256, 512))
    for oz in range(2):
        grow[oz, part, pq * 128 + (2 * half + py) * 32 + oz * 16 + pz] = 1.0
    return shrink, grow


def body(n, levels, vorticity, shift_field, new_index, parent_slot, flags):
    blocks, cells = vorticity.shape[2:]
    vort, shift = vorticity[0], shift_field[0]
    tab = jnp.concatenate([new_index, parent_slot, flags], axis=1)
    tab = jnp.pad(tab, ((0, 0), (0, 128 - 3 * blocks)))
    any_space = pl.BlockSpec(memory_space=pl.ANY)
    vmem = pl.BlockSpec(memory_space=pltpu.VMEM)
    smem = pl.BlockSpec(memory_space=pltpu.SMEM)
    bf16 = jnp.bfloat16
    shape = jax.ShapeDtypeStruct
    dma = pltpu.SemaphoreType.DMA
    height = cells // 128

    below_v, below_s, above_v, above_s, tables = pl.pallas_call(
        functools.partial(share_kernel, n, levels),
        out_shape=(
            shape((3, blocks, HALO), bf16), shape((blocks, HALO), bf16),
            shape((3, blocks, HALO), bf16), shape((blocks, HALO), bf16),
            shape((2, n, 1, 128), jnp.int32),
        ),
        in_specs=[vmem, any_space, any_space],
        out_specs=(any_space, any_space, any_space, any_space, vmem),
        scratch_shapes=[dma((n,)), dma((n,)), dma((n,)), dma((n,)), dma((4,)), dma((4,))],
        compiler_params=pltpu.CompilerParams(collective_id=0, has_side_effects=True),
        name="share",
    )(tab, vort, shift)

    shrink, grow = selection_tables()
    send, ghost = pl.pallas_call(
        functools.partial(remesh_kernel, n),
        out_shape=(
            shape((n, CAP, 3, height, 128), bf16),
            shape((n, CAP, 3, 32, 128), bf16),
        ),
        in_specs=[smem] + [vmem] * 7,
        out_specs=(vmem, vmem),
        scratch_shapes=[pltpu.VMEM((3, height * blocks, 128), jnp.float32)],
        compiler_params=pltpu.CompilerParams(vmem_limit_bytes=VMEM_LIMIT),
        name="remesh",
    )(tables, vort, shift, below_v, below_s, above_v, above_s, jnp.asarray(shrink, bf16))

    got, got_ghost = pl.pallas_call(
        functools.partial(exchange_kernel, n, levels),
        out_shape=(shape(send.shape, bf16), shape(ghost.shape, bf16)),
        in_specs=[any_space] * 2,
        out_specs=(any_space,) * 2,
        scratch_shapes=[dma((n,)), dma((n,)), dma((n,)), dma((n,))],
        compiler_params=pltpu.CompilerParams(collective_id=1, has_side_effects=True),
        name="exchange",
    )(send, ghost)

    out = pl.pallas_call(
        functools.partial(settle_kernel, n, levels),
        out_shape=shape((3, blocks, cells), bf16),
        in_specs=[smem] + [vmem] * 4,
        out_specs=vmem,
        scratch_shapes=[pltpu.VMEM((3, height * blocks, 128), jnp.float32)],
        compiler_params=pltpu.CompilerParams(vmem_limit_bytes=VMEM_LIMIT),
        name="settle",
    )(tables, send, got, got_ghost, jnp.asarray(grow, bf16))
    return out[None]


def solution(mesh):
    placed = (
        P("lvl", None, "blk", None),
        P("lvl", "blk", None),
        P("lvl", "blk"),
        P("lvl", "blk"),
        P("lvl", "blk"),
    )
    step = functools.partial(body, mesh.shape["blk"], mesh.shape["lvl"])
    return jax.shard_map(
        step, mesh=mesh, in_specs=placed, out_specs=P("lvl", None, "blk", None), check_vma=False
    )
```

profile of v0, /device:TPU:1, one launch (start us, length us, event | category | flops | bytes accessed | tf_op | source)
XLA Modules:
  0.0 74.4 jit_solution(14622868908668996732)
XLA Ops:
  0.0 0.8 %pad_add_fusion = s32[1,24]{1,0:T(1,128)S(1)} fusion(s32[1,8]{1,0:T(1,128)} %param.11, s32[1,8]{1,0:T(1,128)} %param.10, s32[1,8]{1,0:T(1,128)} %param.9), kind=kLoop, calls=%fused_computation | loop fusion | flops 48 | bytes 192 | tf_op jit(solution)/shard_map/concatenate | solution.py:366
  0.8 0.5 pad.4.tab
  1.3 10.6 %share.1 = (bf16[3,8,2048]{2,1,0:T(8,128)(2,1)}, bf16[8,2048]{1,0:T(8,128)(2,1)}, bf16[3,8,2048]{2,1,0:T(8,128)(2,1)}, bf16[8,2048]{1,0:T(8,128)(2,1)}, s32[2,8,1,128]{3,2,1,0:T(1,128)}) custom-call(s32[1,128]{1,0:T(1,128)} %pad.4.tab, bf16[3,8,32768]{2,1,0:T(8,128)(2,1)} %bitcast.3, bf16[8,32768]{1,0:T(8,128)(2,1)} %bitcast.5), custom_call_target="tpu_custom_call" | custom-call | tf_op jit(solution)/shard_map/share/pallas_call | solution.py:376
  11.9 6.3 %remesh.1 = (bf16[8,2,3,256,128]{4,3,2,1,0:T(8,128)(2,1)}, bf16[8,2,3,32,128]{4,3,2,1,0:T(8,128)(2,1)}) custom-call(s32[2,8,1,128]{3,2,1,0:T(1,128)} %get-tuple-element.14.tables, bf16[3,8,32768]{2,1,0:T(8,128)(2,1)} %bitcast.4, bf16[8,32768]{1,0:T(8,128)(2,1)} %bitcast.6, bf16[3,8,2048]{2,1,0:T(8,128)(2,1)} %get-tuple-element.15.below_v, ...), custom_call_target="tpu_custom_call" | custom-call | tf_op jit(solution)/shard_map/remesh/pallas_call | solution.py:391
  18.2 44.2 %exchange.1 = (bf16[8,2,3,256,128]{4,3,2,1,0:T(8,128)(2,1)}, bf16[8,2,3,32,128]{4,3,2,1,0:T(8,128)(2,1)}) custom-call(bf16[8,2,3,256,128]{4,3,2,1,0:T(8,128)(2,1)} %get-tuple-element.19.send, bf16[8,2,3,32,128]{4,3,2,1,0:T(8,128)(2,1)} %get-tuple-element.20.ghost), custom_call_target="tpu_custom_call" | custom-call | tf_op jit(solution)/shard_map/exchange/pallas_call | solution.py:404
  62.5 11.9 %settle.1 = bf16[3,8,32768]{2,1,0:T(8,128)(2,1)} custom-call(s32[2,8,1,128]{3,2,1,0:T(1,128)} %get-tuple-element.14.tables, bf16[8,2,3,256,128]{4,3,2,1,0:T(8,128)(2,1)} %get-tuple-element.19.send, bf16[8,2,3,256,128]{4,3,2,1,0:T(8,128)(2,1)} %get-tuple-element.21.got, bf16[8,2,3,32,128]{4,3,2,1,0:T(8,128)(2,1)} %get-tuple-element.22.got_ghost, ...), custom_call_target="tpu_custom_call" | custom-call | tf_op jit(solution)/shard_map/settle/pallas_call | solution.py:414
where the time goes:
time: 74.6 us; the launch traced here: 74.4 us
  Pallas kernels  73.1 us (98%)
  other arithmetic  0.76 us (1%)
    pallas_call x1, Pallas kernels, body(): pl.pallas_call(functools.partial(exchange_kernel, n, levels), out_shape=(...  44.2 us
    pallas_call x1, Pallas kernels, body(): pl.pallas_call(functools.partial(settle_kernel, n, levels), out_shape=sha...  11.9 us
    pallas_call x1, Pallas kernels, body(): pl.pallas_call(functools.partial(share_kernel, n, levels), out_shape=(sha...  10.6 us
    pallas_call x1, Pallas kernels, body(): pl.pallas_call(functools.partial(remesh_kernel, n), out_shape=(shape((n,...  6.31 us

commit v1 on v0

v1 whole, which is shorter than its diff:
```python
import functools

import jax
import jax.numpy as jnp
import numpy as np
from jax import lax
from jax.experimental import pallas as pl
from jax.experimental.pallas import tpu as pltpu
from jax.sharding import PartitionSpec as P

MESH = pl.DeviceIdType.MESH
EDGE = 32
PLANE = EDGE * EDGE
HALO = 2 * PLANE
CAP = 2
VMEM_LIMIT = 60 * 1024 * 1024


def device(blk, lvl):
    return {"blk": blk, "lvl": lvl}


def enter(n, levels, me, lvl):
    barrier = pltpu.get_barrier_semaphore()

    def greet(blk, level):
        pl.semaphore_signal(barrier, inc=1, device_id=device(blk, level), device_id_type=MESH)

    for k in range(1, n):
        greet(lax.rem(me + k, n), lvl)

    @pl.when(lvl > 0)
    def _():
        for k in range(n):
            greet(lax.rem(me + k, n), lvl - 1)

    @pl.when(lvl < levels - 1)
    def _():
        for k in range(n):
            greet(lax.rem(me + k, n), lvl + 1)

    pl.semaphore_wait(
        barrier, n - 1 + n * ((lvl > 0).astype(jnp.int32) + (lvl < levels - 1).astype(jnp.int32))
    )


def remote(src, dst, send, recv, target):
    return pltpu.make_async_remote_copy(
        src_ref=src, dst_ref=dst, send_sem=send, recv_sem=recv, device_id=target, device_id_type=MESH
    )


def tap_weights(shifts):
    size = jnp.abs(shifts)
    rest = 1.0 - size
    size2 = size * size
    rest2 = rest * rest
    middle = 1.0 + size2 * (1.5 * size - 2.5)
    ahead = 1.0 + rest2 * (1.5 * rest - 2.5)
    behind = -0.5 * rest2 * size
    far = -0.5 * size2 * rest
    up = shifts >= 0.0
    return {
        -2: jnp.where(up, 0.0, far),
        -1: jnp.where(up, behind, ahead),
        0: middle,
        1: jnp.where(up, ahead, behind),
        2: jnp.where(up, far, 0.0),
    }


def picks(keys, wanted):
    count, first, second = jnp.int32(0), jnp.int32(0), jnp.int32(0)
    for b, key in enumerate(keys):
        hit = key == wanted
        first = jnp.where(jnp.logical_and(hit, count == 0), b, first)
        second = jnp.where(jnp.logical_and(hit, count == 1), b, second)
        count = count + hit.astype(jnp.int32)
    return first, second


def move_kernel(n, levels, spots, tab, vort, shift, shrink,
                got0, got1, got2, got_ghost, tables,
                send0, send1, send2, ghost, below_v, below_s, above_v, above_s, rows, whole, small, local,
                near_s, near_r, coarse_s, coarse_r, halo_s, halo_r, block_s, block_r, ghost_s, ghost_r,
                own_sem, table_sem):
    me = lax.axis_index("blk")
    lvl = lax.axis_index("lvl")
    blocks, cells = vort.shape[1:]
    lane_tiles = PLANE // 128
    height = cells // 128
    quarter = height // 4
    coarse_level = jnp.maximum(lvl - 1, 0)
    got, send = (got0, got1, got2), (send0, send1, send2)
    after = device(lax.rem(me + 1, n), lvl)
    before = device(lax.rem(me + n - 1, n), lvl)
    enter(n, levels, me, lvl)

    def high(target):
        part = pl.ds(cells - HALO, HALO)
        return (
            remote(vort.at[:, :, part], below_v, halo_s.at[0], halo_r.at[0], target),
            remote(shift.at[:, part], below_s, halo_s.at[1], halo_r.at[1], target),
        )

    def low(target):
        part = pl.ds(0, HALO)
        return (
            remote(vort.at[:, :, part], above_v, halo_s.at[2], halo_r.at[2], target),
            remote(shift.at[:, part], above_s, halo_s.at[3], halo_r.at[3], target),
        )

    def near(k):
        return remote(tab, tables.at[0, me], near_s.at[k], near_r.at[k], device(lax.rem(me + k, n), lvl))

    def coarse(k):
        return remote(tab, tables.at[1, me], coarse_s.at[k], coarse_r.at[k],
                      device(lax.rem(me + k, n), coarse_level))

    @pl.when(me < n - 1)
    def _():
        for copy in high(after):
            copy.start()

    @pl.when(me > 0)
    def _():
        for copy in low(before):
            copy.start()

    for k in range(1, n):
        near(k).start()

    @pl.when(lvl > 0)
    def _():
        for k in range(n):
            coarse(k).start()

    tables[0, me] = tab[...]
    owners = [lax.div(spots[0, b], blocks) for b in range(blocks)]

    @pl.when(me < n - 1)
    def _():
        for copy in low(after):
            copy.wait_recv()

    @pl.when(me > 0)
    def _():
        for copy in high(before):
            copy.wait_recv()

    sublane = lax.broadcasted_iota(jnp.int32, (blocks, 128), 0)

    def tile(ref, c, at):
        part = ref[c, :, pl.ds(at, 128)] if c is not None else ref[:, pl.ds(at, 128)]
        return part.astype(jnp.float32)

    def source_tile(own, below, above, c, x, j):
        if 0 <= x < EDGE:
            return tile(own, c, pl.multiple_of(x * PLANE + j * 128, 128))
        if x < 0:
            inner = pltpu.roll(tile(own, c, pl.multiple_of((EDGE + x) * PLANE + j * 128, 128)), 1, 0)
            outer = pltpu.roll(tile(below, c, pl.multiple_of((2 + x) * PLANE + j * 128, 128)), 1, 0)
            outer = jnp.where(me == 0, 0.0, outer)
            return jnp.where(sublane == 0, outer, inner)
        at = pl.multiple_of((x - EDGE) * PLANE + j * 128, 128)
        inner = pltpu.roll(tile(own, c, at), blocks - 1, 0)
        outer = pltpu.roll(tile(above, c, at), blocks - 1, 0)
        outer = jnp.where(me == n - 1, 0.0, outer)
        return jnp.where(sublane == blocks - 1, outer, inner)

    def remesh(c):
        def chunk(j, carry):
            sums = {}
            for x in range(-2, EDGE + 2):
                weights = tap_weights(source_tile(shift, below_s, above_s, None, x, j))
                value = source_tile(vort, below_v, above_v, c, x, j)
                for offset in range(-2, 3):
                    to = x + offset
                    if 0 <= to < EDGE:
                        term = value * weights[offset]
                        sums[to] = sums[to] + term if to in sums else term
                done = x - 2
                if 0 <= done < EDGE:
                    at = pl.multiple_of((done * lane_tiles + j) * blocks, blocks)
                    rows[pl.ds(at, blocks), :] = sums.pop(done)
            return carry

        lax.fori_loop(0, lane_tiles, chunk, 0)
        for b in range(blocks):
            whole[b] = rows[pl.ds(b, height, stride=blocks), :].astype(jnp.bfloat16)

    def block_copy(c, k):
        to = lax.rem(me + k, n)
        return remote(send[c].at[to], got[c].at[me], block_s.at[c, k], block_r.at[c, k], device(to, lvl))

    def own_copy(c):
        return pltpu.make_async_copy(send[c].at[me], got[c].at[me], own_sem.at[c])

    def ghost_copy(c, k):
        to = lax.rem(me + k, n)
        return remote(ghost.at[c, to], got_ghost.at[c, me], ghost_s.at[c, k], ghost_r.at[c, k],
                      device(to, coarse_level))

    def send_blocks(c):
        def pack(k, carry):
            to = lax.rem(me + k, n)
            first, second = picks(owners, to)
            send[c][to, 0] = whole[first]
            send[c][to, 1] = whole[second]
            return carry

        lax.fori_loop(1, n + 1, pack, 0)
        for k in range(1, n):
            block_copy(c, k).start()
        own_copy(c).start()

    def restrict(c):
        for b in range(blocks):
            block = whole[b]
            wide = jnp.concatenate([block[q * quarter:(q + 1) * quarter] for q in range(4)], axis=1)
            pairs = jnp.dot(wide, shrink[...], preferred_element_type=jnp.float32)
            pairs = pairs.reshape(4, 2, 8, 128)
            small[c, b] = (pairs[:, 0] + pairs[:, 1]).reshape(32, 128).astype(jnp.bfloat16)

    def send_ghosts(c, parents):
        def pack(k, carry):
            to = lax.rem(me + k, n)
            first, second = picks(parents, to)
            ghost[c, to, 0] = small[c, first]
            ghost[c, to, 1] = small[c, second]
            return carry

        lax.fori_loop(0, n, pack, 0)

        @pl.when(lvl > 0)
        def _():
            for k in range(n):
                ghost_copy(c, k).start()

    remesh(0)
    send_blocks(0)

    for k in range(1, n):
        source = lax.rem(me + n - k, n)
        remote(tab, tables.at[0, source], near_s.at[k], near_r.at[k], before).wait_recv()
    fetch = pltpu.make_async_copy(tables.at[0], local, table_sem)
    fetch.start()
    restrict(0)
    fetch.wait()
    parents = []
    for b in range(blocks):
        home, spot = lax.div(spots[0, b], blocks), lax.rem(spots[0, b], blocks)
        parents.append(lax.div(local[home, 0, blocks + spot], 8 * blocks))
    send_ghosts(0, parents)
    remesh(1)
    send_blocks(1)
    restrict(1)
    send_ghosts(1, parents)
    remesh(2)
    restrict(2)
    send_ghosts(2, parents)
    send_blocks(2)

    @pl.when(lvl > 0)
    def _():
        for k in range(n):
            coarse(k).wait_send()
            for c in range(3):
                ghost_copy(c, k).wait_send()

    @pl.when(lvl < levels - 1)
    def _():
        for k in range(n):
            source = lax.rem(me + n - k, n)
            remote(tab, tables.at[1, source], coarse_s.at[k], coarse_r.at[k], before).wait_recv()

    @pl.when(me < n - 1)
    def _():
        for copy in high(after):
            copy.wait_send()

    @pl.when(me > 0)
    def _():
        for copy in low(before):
            copy.wait_send()

    for k in range(1, n):
        near(k).wait_send()
    for c in range(3):
        own_copy(c).wait()
        for k in range(1, n):
            source = lax.rem(me + n - k, n)
            remote(send[c].at[me], got[c].at[source], block_s.at[c, k], block_r.at[c, k], before).wait_recv()
            block_copy(c, k).wait_send()

    @pl.when(lvl < levels - 1)
    def _():
        for c in range(3):
            for k in range(n):
                source = lax.rem(me + n - k, n)
                remote(ghost.at[c, me], got_ghost.at[c, source], ghost_s.at[c, k], ghost_r.at[c, k],
                       before).wait_recv()


def settle_kernel(n, levels, tables, got0, got1, got2, got_ghost, grow, out, rows):
    me = lax.axis_index("blk")
    lvl = lax.axis_index("lvl")
    blocks = out.shape[1]
    height = rows.shape[1] // blocks

    def place(e, count):
        source = lax.div(e, blocks)
        b = lax.rem(e, blocks)
        count = jnp.where(b == 0, 0, count)
        position = tables[0, source, 0, b]
        mine = lax.div(position, blocks) == me
        spot = lax.rem(position, blocks)

        @pl.when(mine)
        def _():
            for c, got in enumerate((got0, got1, got2)):
                rows[c, pl.ds(spot, height, stride=blocks), :] = got[source, count].astype(jnp.float32)

        return count + mine.astype(jnp.int32)

    lax.fori_loop(0, n * blocks, place, jnp.int32(0))

    row = lax.broadcasted_iota(jnp.int32, (32, 32), 0)
    column = lax.broadcasted_iota(jnp.int32, (32, 32), 1)
    mask_row = lax.broadcasted_iota(jnp.int32, (32, 128), 0)
    mask_lane = lax.broadcasted_iota(jnp.int32, (32, 128), 1)

    def refine(e, count):
        source = lax.div(e, blocks)
        b = lax.rem(e, blocks)
        count = jnp.where(b == 0, 0, count)
        position = tables[1, source, 0, b]
        home = lax.div(position, blocks)
        local = lax.rem(position, blocks)
        parent = tables[1, home, 0, blocks + local]
        flag = tables[1, home, 0, 2 * blocks + local]
        mine = lax.div(parent, 8 * blocks) == me

        @pl.when(jnp.logical_and(mine, flag == 1))
        def _():
            code = lax.rem(parent, 8 * blocks)
            spot = lax.div(code, 8)
            ox = lax.rem(lax.div(code, 4), 2)
            oy = lax.rem(lax.div(code, 2), 2)
            oz = lax.rem(code, 2)
            spread = []
            for half in range(2):
                hot = jnp.logical_and(row // 8 == column // 8,
                                      column % 8 == 2 * (row % 8 - 4 * oy) + half)
                spread.append(hot.astype(jnp.float32).astype(jnp.bfloat16))
            mask = jnp.logical_and(mask_row % 8 // 4 == oy, mask_lane % 32 // 16 == oz)
            for c in range(3):
                block = got_ghost[c, source, count]
                wide = jnp.concatenate(
                    [jnp.dot(part, block, preferred_element_type=jnp.float32) for part in spread], axis=1
                ).astype(jnp.bfloat16)
                full = jnp.dot(wide, grow[oz], preferred_element_type=jnp.float32)
                for q in range(4):
                    where = pl.ds((ox * 128 + q * 32) * blocks + spot, 32, stride=blocks)
                    rows[c, where, :] = jnp.where(
                        mask, full[:, q * 128:(q + 1) * 128], rows[c, where, :]
                    )

        return count + mine.astype(jnp.int32)

    lax.fori_loop(0, jnp.where(lvl < levels - 1, n * blocks, 0), refine, jnp.int32(0))

    def finish(r, carry):
        for c in range(3):
            for step in range(8):
                at = r * 8 + step
                out[c, :, pl.ds(pl.multiple_of(at * 128, 128), 128)] = rows[
                    c, pl.ds(pl.multiple_of(at * blocks, blocks), blocks), :
                ].astype(jnp.bfloat16)
        return carry

    lax.fori_loop(0, height // 8, finish, 0)


def selection_tables():
    src = np.arange(512)
    to = np.arange(128)
    q, y, z = src // 128, src % 128 // 32, src % 32
    target = q * 32 + (y // 2) * 16 + z // 2
    shrink = np.where(target[:, None] == to[None, :], 0.125, 0.0)
    part = np.arange(256)
    half, pq, py, pz = part // 128, part % 128 // 32, part % 32 // 16, part % 16
    grow = np.zeros((2, 256, 512))
    for oz in range(2):
        grow[oz, part, pq * 128 + (2 * half + py) * 32 + oz * 16 + pz] = 1.0
    return shrink, grow


def body(n, levels, vorticity, shift_field, new_index, parent_slot, flags):
    blocks, cells = vorticity.shape[2:]
    vort, shift = vorticity[0], shift_field[0]
    tab = jnp.concatenate([new_index, parent_slot, flags], axis=1)
    tab = jnp.pad(tab, ((0, 0), (0, 128 - 3 * blocks)))
    any_space = pl.BlockSpec(memory_space=pl.ANY)
    vmem = pl.BlockSpec(memory_space=pltpu.VMEM)
    smem = pl.BlockSpec(memory_space=pltpu.SMEM)
    bf16 = jnp.bfloat16
    shape = jax.ShapeDtypeStruct
    dma = pltpu.SemaphoreType.DMA
    height = cells // 128

    shrink, grow = selection_tables()
    many = shape((n, CAP, height, 128), bf16)
    vm = pltpu.VMEM
    got0, got1, got2, got_ghost, tables = pl.pallas_call(
        functools.partial(move_kernel, n, levels),
        out_shape=(many, many, many, shape((3, n, CAP, 32, 128), bf16), shape((2, n, 1, 128), jnp.int32)),
        in_specs=[smem, vmem, vmem, vmem, vmem],
        out_specs=(any_space,) * 4 + (vmem,),
        scratch_shapes=[
            vm(many.shape, bf16), vm(many.shape, bf16), vm(many.shape, bf16),
            vm((3, n, CAP, 32, 128), bf16),
            vm((3, blocks, HALO), bf16), vm((blocks, HALO), bf16),
            vm((3, blocks, HALO), bf16), vm((blocks, HALO), bf16),
            vm((height * blocks, 128), jnp.float32), vm((blocks, height, 128), bf16),
            vm((3, blocks, 32, 128), bf16), pltpu.SMEM((n, 1, 128), jnp.int32),
            dma((n,)), dma((n,)), dma((n,)), dma((n,)), dma((4,)), dma((4,)),
            dma((3, n)), dma((3, n)), dma((3, n)), dma((3, n)), dma((3,)), dma,
        ],
        compiler_params=pltpu.CompilerParams(
            collective_id=0, has_side_effects=True, vmem_limit_bytes=VMEM_LIMIT
        ),
        name="move",
    )(new_index, tab, vort, shift, jnp.asarray(shrink, bf16))

    out = pl.pallas_call(
        functools.partial(settle_kernel, n, levels),
        out_shape=shape((3, blocks, cells), bf16),
        in_specs=[smem] + [vmem] * 5,
        out_specs=vmem,
        scratch_shapes=[pltpu.VMEM((3, height * blocks, 128), jnp.float32)],
        compiler_params=pltpu.CompilerParams(vmem_limit_bytes=VMEM_LIMIT),
        name="settle",
    )(tables, got0, got1, got2, got_ghost, jnp.asarray(grow, bf16))
    return out[None]


def solution(mesh):
    placed = (
        P("lvl", None, "blk", None),
        P("lvl", "blk", None),
        P("lvl", "blk"),
        P("lvl", "blk"),
        P("lvl", "blk"),
    )
    step = functools.partial(body, mesh.shape["blk"], mesh.shape["lvl"])
    return jax.shard_map(
        step, mesh=mesh, in_specs=placed, out_specs=P("lvl", None, "blk", None), check_vma=False
    )
```

time: 74.6 us -> 66.6 us (0.89)
  Pallas kernels: 73.1 us -> 65 us
    pallas_call x3 -> x1, Pallas kernels: 61.2 us -> 54.4 us  [body(): pl.pallas_call(functools.partial(move_kernel, n, levels), out_shape=(many...]
    pallas_call x1, Pallas kernels: 11.9 us -> 10.6 us  [body(): pl.pallas_call(functools.partial(settle_kernel, n, levels), out_shape=sha...]
where the time goes in v1:
time: 66.6 us; the launch traced here: 66.3 us
  Pallas kernels  65 us (98%)
  other arithmetic  0.76 us (1%)
    pallas_call x1, Pallas kernels, body(): pl.pallas_call(functools.partial(move_kernel, n, levels), out_shape=(many...  54.4 us
    pallas_call x1, Pallas kernels, body(): pl.pallas_call(functools.partial(settle_kernel, n, levels), out_shape=sha...  10.6 us

profile of v1, /device:TPU:1, one launch (start us, length us, event | category | flops | bytes accessed | tf_op | source)
XLA Modules:
  0.0 66.3 jit_solution(15889905145867817356)
XLA Ops:
  0.0 0.8 %pad_add_fusion = s32[1,24]{1,0:T(1,128)S(1)} fusion(s32[1,8]{1,0:T(1,128)} %param.11, s32[1,8]{1,0:T(1,128)} %param.10, s32[1,8]{1,0:T(1,128)} %spots.1), kind=kLoop, calls=%fused_computation | loop fusion | flops 48 | bytes 192 | tf_op jit(solution)/shard_map/concatenate | solution.py:402
  0.8 0.5 pad.4.tab
  1.3 54.4 %move.1 = (bf16[8,2,256,128]{3,2,1,0:T(8,128)(2,1)}, bf16[8,2,256,128]{3,2,1,0:T(8,128)(2,1)}, bf16[8,2,256,128]{3,2,1,0:T(8,128)(2,1)}, bf16[3,8,2,32,128]{4,3,2,1,0:T(8,128)(2,1)}, s32[2,8,1,128]{3,2,1,0:T(1,128)}) custom-call(s32[1,8]{1,0:T(1,128)} %spots.1, s32[1,128]{1,0:T(1,128)} %pad.4.tab, bf16[3,8,32768]{2,1,0:T(8,128)(2,1)} %bitcast.3, ...), custom_call_target="tpu_custom_call" | custom-call | tf_op jit(solution)/shard_map/move/pallas_call | solution.py:415
  55.7 10.6 %settle.1 = bf16[3,8,32768]{2,1,0:T(8,128)(2,1)} custom-call(s32[2,8,1,128]{3,2,1,0:T(1,128)} %get-tuple-element.10.tables, bf16[8,2,256,128]{3,2,1,0:T(8,128)(2,1)} %get-tuple-element.11.got0, bf16[8,2,256,128]{3,2,1,0:T(8,128)(2,1)} %get-tuple-element.12.got1, bf16[8,2,256,128]{3,2,1,0:T(8,128)(2,1)} %get-tuple-element.13.got2, ...), custom_call_target="tpu_custom_call" | custom-call | tf_op jit(solution)/shard_map/settle/pallas_call | solution.py:436
